TPU v7x, 32 devices: a whole 2x2x4 slice. The times are simulated.
32 devices in a mesh: gx: 4 (over y, x), gy: 8 (over z, core).
Axes of the slice: x: 2, y: 2, z: 4, core: 2. Of those that a mesh axis runs over, the one named last changes fastest.
Arguments:
- cotangent: float32 [128, 512, 128], P('gx', 'gy'), may hold values from -6 to 6
- speed: float32 [3, 128, 512, 128], P(None, 'gx', 'gy'), may hold values from 0.05 to 0.45
- coeff: float32 [3, 128, 512, 128], P(None, 'gx', 'gy'), may hold values from 0.3 to 3
- dirs: int32 [3, 128, 512], P(None, 'gx', 'gy'), may hold values from 0 to 1
Outputs:
- grad: float32 [128, 512, 128], P('gx', 'gy')
Inputs may be any that keep to these rules, and one draw needn't show every extreme that they name: `dirs`: 0 means the lower cell of a face is upwind, 1 the upper cell.
All inputs are finite; a program needn't handle non-finite values.
Results may differ from a plain program's by a relative error of at most 0.0003.
Values sent between devices are 32-bit elements; how exact they have to be, the bound alone decides.
A program may use at most 128 MiB of HBM per device.

v0:
```python
import jax
import jax.numpy as jnp
from jax import lax
from jax.sharding import PartitionSpec as P

ITERS = 2


explicit_table = (
    (0.0, 0.0, 0.0, 0.0),
    (0.5, 0.0, 0.0, 0.0),
    (0.25, 0.5, 0.0, 0.0),
    (0.2, 0.3, 0.5, 0.0),
)
implicit_table = (
    (0.0, 0.0, 0.0, 0.0),
    (0.25, 0.25, 0.0, 0.0),
    (0.25, 0.25, 0.25, 0.0),
    (0.15, 0.35, 0.25, 0.25),
)
section_weights = (0.15, 0.35, 0.25, 0.25)
implicit_diagonal = 0.25
step_length = 1.0


def passed_along(value, axis, steps):
    count = lax.axis_size(axis)
    leading, last = (max(0, -steps), min(count, count - steps))
    return lax.ppermute(value, axis, [(source, source + steps) for source in range(leading, last)])


def local_ahead(values, dimension):
    tail = lax.slice_in_dim(values, 1, values.shape[dimension], axis=dimension)
    return jnp.concatenate(
        [tail, jnp.zeros_like(lax.slice_in_dim(values, 0, 1, axis=dimension))], dimension
    )


def local_behind(values, dimension):
    head = lax.slice_in_dim(values, 0, values.shape[dimension] - 1, axis=dimension)
    return jnp.concatenate(
        [jnp.zeros_like(lax.slice_in_dim(values, 0, 1, axis=dimension)), head], dimension
    )


def with_plane_after(values, plane, dimension):
    tail = lax.slice_in_dim(values, 1, values.shape[dimension], axis=dimension)
    return jnp.concatenate([tail, plane], dimension)


def with_plane_before(values, plane, dimension):
    head = lax.slice_in_dim(values, 0, values.shape[dimension] - 1, axis=dimension)
    return jnp.concatenate([plane, head], dimension)


def apply_returned(fields, coeff, velocity):
    count = fields.shape[0]
    from_above_x = passed_along(fields[:, :1], "gx", -1)
    from_above_y = passed_along(fields[:, :, :1], "gy", -1)
    aheads = (
        with_plane_after(fields, from_above_x, 1),
        with_plane_after(fields, from_above_y, 2),
        local_ahead(fields, 3),
    )
    diffused = fields[count - 1]
    total = jnp.zeros_like(diffused)
    outgoing = []
    for dimension in range(3):
        ahead = aheads[dimension]
        flux = coeff[dimension] * (ahead[count - 1] - diffused)
        members = [flux]
        if count == 2:
            moved = velocity[dimension] * (ahead[0] - fields[0])
            upwind_here = velocity[dimension] > 0
            total = total + jnp.where(upwind_here, moved, 0.0)
            members.append(jnp.where(upwind_here, 0.0, moved))
        total = total + flux
        outgoing.append(jnp.stack(members))
    from_below_x = passed_along(outgoing[0][:, -1:], "gx", 1)
    from_below_y = passed_along(outgoing[1][:, :, -1:], "gy", 1)
    behinds = (
        with_plane_before(outgoing[0], from_below_x, 1),
        with_plane_before(outgoing[1], from_below_y, 2),
        local_behind(outgoing[2], 3),
    )
    for dimension in range(3):
        behind = behinds[dimension]
        total = total - behind[0]
        if count == 2:
            total = total + behind[1]
    return total


def paired_products(residual, image):
    return lax.psum((jnp.sum(residual * residual), jnp.sum(residual * image)), ("gx", "gy"))


def local(cotangent, speed, coeff, dirs):
    signs = (1 - 2 * dirs).astype(jnp.float32)
    velocity = speed * signs[..., None]

    def operate(fields):
        return apply_returned(fields, coeff, velocity)

    def section_operator(values):
        return values - implicit_diagonal * step_length * operate(values[None])

    section_adjoints = [None, None, None, None]
    for section_index in (3, 2, 1, 0):
        advected = step_length * section_weights[section_index] * cotangent
        diffused = step_length * section_weights[section_index] * cotangent
        for later in range(section_index + 1, 4):
            advected = (
                advected
                + step_length * explicit_table[later][section_index] * section_adjoints[later]
            )
            diffused = (
                diffused
                + step_length * implicit_table[later][section_index] * section_adjoints[later]
            )
        source = operate(jnp.stack([advected, diffused]))
        if section_index > 0:
            solution = jnp.zeros_like(source)
            residual = source
            image = section_operator(residual)
            norm_now, product = paired_products(residual, image)
            alpha = norm_now / product
            direction = residual
            along = image
            for iteration in range(ITERS):
                solution = solution + alpha * direction
                residual = residual - alpha * along
                if iteration + 1 < ITERS:
                    image = section_operator(residual)
                    norm_next, product = paired_products(residual, image)
                    ratio = norm_next / norm_now
                    alpha = norm_next / (product - ratio * norm_next / alpha)
                    direction = residual + ratio * direction
                    along = image + ratio * along
                    norm_now = norm_next
            section_adjoints[section_index] = solution
        else:
            section_adjoints[section_index] = source
    return (
        cotangent
        + section_adjoints[0]
        + section_adjoints[1]
        + section_adjoints[2]
        + section_adjoints[3]
    )


def solution(mesh):
    return jax.shard_map(
        local,
        mesh=mesh,
        in_specs=(
            P("gx", "gy", None),
            P(None, "gx", "gy", None),
            P(None, "gx", "gy", None),
            P(None, "gx", "gy"),
        ),
        out_specs=P("gx", "gy", None),
        check_vma=False,
    )
```

profile of v0, /device:TPU:1, one launch (start us, length us, event | category | flops | bytes accessed | tf_op | source)
XLA Modules:
  0.0 511.8 jit_solution(1982992677150696999)
XLA Ops:
  13.6 5.2 %collective-permute-start.2 = (f32[2,1,64,128]{3,2,1,0:T(8,128)S(1)}, f32[2,1,64,128]{3,2,1,0:T(8,128)S(1)}, u32[]{:S(2)}, u32[]{:S(2)}) collective-permute-start(f32[2,1,64,128]{3,2,1,0:T(8,128)S(1)} %pad_maximum_fusion.19), channel_id=1, source_target_pairs={{0,8},{8,16},{16,24},{1,9},{9,17},{17,25},{2,10},{10,18},{18,26},{... | collective-permute-start | bytes 196616 | tf_op jit(solution)/shard_map/ppermute | solution.py:29
  18.8 3.9 collective-permute-start.3
  36.6 4.6 collective-permute-start.6
  47.7 39.7 %all-reduce.25 = (f32[]{:T(128)}, f32[]{:T(128)}) all-reduce(f32[]{:T(128)} %get-tuple-element.16, f32[]{:T(128)} %get-tuple-element.15), channel_id=1, replica_groups=mesh['gx'=4,'gy'=8] {'gx','gy'}, use_global_device_ids=true, to_apply=%region_1.2 | all-reduce | flops 2 | bytes 16 | tf_op jit(solution)/shard_map/psum | solution.py:95
  100.4 4.5 collective-permute-start.10
  111.3 39.3 %all-reduce.24 = (f32[]{:T(128)}, f32[]{:T(128)}) all-reduce(f32[]{:T(128)} %get-tuple-element.14, f32[]{:T(128)} %get-tuple-element.13), channel_id=1, replica_groups=mesh['gx'=4,'gy'=8] {'gx','gy'}, use_global_device_ids=true, to_apply=%region_5.6 | all-reduce | flops 2 | bytes 16 | tf_op jit(solution)/shard_map/psum | solution.py:95
  169.8 4.5 select_bitcast_fusion.8
  174.3 4.8 collective-permute-start.14
  186.7 4.6 fusion.87
  199.2 4.3 collective-permute-start.18
  208.5 39.3 %all-reduce.23 = (f32[]{:T(128)}, f32[]{:T(128)}) all-reduce(f32[]{:T(128)} %get-tuple-element.12, f32[]{:T(128)} %get-tuple-element.11), channel_id=1, replica_groups=mesh['gx'=4,'gy'=8] {'gx','gy'}, use_global_device_ids=true, to_apply=%region_9.10 | all-reduce | flops 2 | bytes 16 | tf_op jit(solution)/shard_map/psum | solution.py:95
  260.8 4.5 collective-permute-start.22
  271.7 39.3 %all-reduce.22 = (f32[]{:T(128)}, f32[]{:T(128)}) all-reduce(f32[]{:T(128)} %get-tuple-element.10, f32[]{:T(128)} %get-tuple-element.9), channel_id=1, replica_groups=mesh['gx'=4,'gy'=8] {'gx','gy'}, use_global_device_ids=true, to_apply=%region_13.14 | all-reduce | flops 2 | bytes 16 | tf_op jit(solution)/shard_map/psum | solution.py:95
  331.1 4.5 select_bitcast_fusion.5
  335.7 4.8 collective-permute-start.26
  348.1 4.6 fusion.71
  360.6 4.3 collective-permute-start.30
  369.9 39.3 %all-reduce.21 = (f32[]{:T(128)}, f32[]{:T(128)}) all-reduce(f32[]{:T(128)} %get-tuple-element.8, f32[]{:T(128)} %get-tuple-element.7), channel_id=1, replica_groups=mesh['gx'=4,'gy'=8] {'gx','gy'}, use_global_device_ids=true, to_apply=%region_17.18 | all-reduce | flops 2 | bytes 16 | tf_op jit(solution)/shard_map/psum | solution.py:95
  410.5 3.9 multiply_subtract_fusion
  422.2 4.5 collective-permute-start.34
  426.8 3.9 collective-permute-start.35
  433.1 39.3 %all-reduce.20 = (f32[]{:T(128)}, f32[]{:T(128)}) all-reduce(f32[]{:T(128)} %get-tuple-element.6, f32[]{:T(128)} %get-tuple-element.5), channel_id=1, replica_groups=mesh['gx'=4,'gy'=8] {'gx','gy'}, use_global_device_ids=true, to_apply=%region_21.22 | all-reduce | flops 2 | bytes 16 | tf_op jit(solution)/shard_map/psum | solution.py:95
  496.0 4.8 collective-permute-start.38
  507.0 4.3 fusion.55
  (305 shorter events, 175.5 us)
Async XLA Ops:
  1.3 7.5 %collective-permute-start = (f32[2,1,64,128]{3,2,1,0:T(8,128)S(1)}, f32[2,1,64,128]{3,2,1,0:T(8,128)S(1)}, u32[]{:S(2)}, u32[]{:S(2)}) collective-permute-start(f32[2,1,64,128]{3,2,1,0:T(8,128)S(1)} %fusion.194), channel_id=1, source_target_pairs={{8,0},{16,8},{24,16},{9,1},{17,9},{25,17},{10,2},{18,10},{26,18},{... | collective-permute-start | bytes 196616 | tf_op jit(solution)/shard_map/ppermute | solution.py:29
  2.6 6.2 %collective-permute-start.1 = (f32[2,32,1,128]{3,2,1,0:T(1,128)S(1)}, f32[2,32,1,128]{3,2,1,0:T(1,128)S(1)}, u32[]{:S(2)}, u32[]{:S(2)}) collective-permute-start(f32[2,32,1,128]{3,2,1,0:T(1,128)S(1)} %fusion.198), channel_id=1, source_target_pairs={{1,0},{2,1},{3,2},{4,3},{5,4},{6,5},{7,6},{9,8},{10,9},{11,10},{12... | collective-permute-start | bytes 98312 | tf_op jit(solution)/shard_map/ppermute | solution.py:29
  13.6 10.7 %collective-permute-start.2 = (f32[2,1,64,128]{3,2,1,0:T(8,128)S(1)}, f32[2,1,64,128]{3,2,1,0:T(8,128)S(1)}, u32[]{:S(2)}, u32[]{:S(2)}) collective-permute-start(f32[2,1,64,128]{3,2,1,0:T(8,128)S(1)} %pad_maximum_fusion.19), channel_id=1, source_target_pairs={{0,8},{8,16},{16,24},{1,9},{9,17},{17,25},{2,10},{10,18},{18,26},{... | collective-permute-start | bytes 196616 | tf_op jit(solution)/shard_map/ppermute | solution.py:29
  28.8 7.0 %collective-permute-start.4 = (f32[1,1,64,128]{3,2,1,0:T(8,128)S(1)}, f32[1,1,64,128]{3,2,1,0:T(8,128)S(1)}, u32[]{:S(2)}, u32[]{:S(2)}) collective-permute-start(f32[1,1,64,128]{3,2,1,0:T(8,128)S(1)} %slice.688), channel_id=1, source_target_pairs={{8,0},{16,8},{24,16},{9,1},{17,9},{25,17},{10,2},{18,10},{26,18},{... | collective-permute-start | bytes 98312 | tf_op jit(solution)/shard_map/ppermute | solution.py:29
  36.6 9.2 %collective-permute-start.6 = (f32[1,1,64,128]{3,2,1,0:T(8,128)S(1)}, f32[1,1,64,128]{3,2,1,0:T(8,128)S(1)}, u32[]{:S(2)}, u32[]{:S(2)}) collective-permute-start(f32[1,1,64,128]{3,2,1,0:T(8,128)S(1)} %slice.692), channel_id=1, source_target_pairs={{0,8},{8,16},{16,24},{1,9},{9,17},{17,25},{2,10},{10,18},{18,26},{... | collective-permute-start | bytes 98312 | tf_op jit(solution)/shard_map/ppermute | solution.py:29
  92.5 7.0 %collective-permute-start.8 = (f32[1,1,64,128]{3,2,1,0:T(8,128)S(1)}, f32[1,1,64,128]{3,2,1,0:T(8,128)S(1)}, u32[]{:S(2)}, u32[]{:S(2)}) collective-permute-start(f32[1,1,64,128]{3,2,1,0:T(8,128)S(1)} %slice.698), channel_id=1, source_target_pairs={{8,0},{16,8},{24,16},{9,1},{17,9},{25,17},{10,2},{18,10},{26,18},{... | collective-permute-start | bytes 98312 | tf_op jit(solution)/shard_map/ppermute | solution.py:29
  93.8 5.7 %collective-permute-start.9 = (f32[1,32,1,128]{3,2,1,0:T(1,128)S(1)}, f32[1,32,1,128]{3,2,1,0:T(1,128)S(1)}, u32[]{:S(2)}, u32[]{:S(2)}) collective-permute-start(f32[1,32,1,128]{3,2,1,0:T(1,128)S(1)} %slice.700), channel_id=1, source_target_pairs={{1,0},{2,1},{3,2},{4,3},{5,4},{6,5},{7,6},{9,8},{10,9},{11,10},{12... | collective-permute-start | bytes 49160 | tf_op jit(solution)/shard_map/ppermute | solution.py:29
  100.4 9.0 %collective-permute-start.10 = (f32[1,1,64,128]{3,2,1,0:T(8,128)S(1)}, f32[1,1,64,128]{3,2,1,0:T(8,128)S(1)}, u32[]{:S(2)}, u32[]{:S(2)}) collective-permute-start(f32[1,1,64,128]{3,2,1,0:T(8,128)S(1)} %slice.702), channel_id=1, source_target_pairs={{0,8},{8,16},{16,24},{1,9},{9,17},{17,25},{2,10},{10,18},{18,26},{... | collective-permute-start | bytes 98312 | tf_op jit(solution)/shard_map/ppermute | solution.py:29
  163.9 5.9 %collective-permute-start.12 = (f32[2,1,64,128]{3,2,1,0:T(8,128)S(1)}, f32[2,1,64,128]{3,2,1,0:T(8,128)S(1)}, u32[]{:S(2)}, u32[]{:S(2)}) collective-permute-start(f32[2,1,64,128]{3,2,1,0:T(8,128)S(1)} %fusion.193), channel_id=1, source_target_pairs={{8,0},{16,8},{24,16},{9,1},{17,9},{25,17},{10,2},{18,10},{26,18},{... | collective-permute-start | bytes 196616 | tf_op jit(solution)/shard_map/ppermute | solution.py:29
  174.3 10.7 %collective-permute-start.14 = (f32[2,1,64,128]{3,2,1,0:T(8,128)S(1)}, f32[2,1,64,128]{3,2,1,0:T(8,128)S(1)}, u32[]{:S(2)}, u32[]{:S(2)}) collective-permute-start(f32[2,1,64,128]{3,2,1,0:T(8,128)S(1)} %pad_maximum_fusion.18), channel_id=1, source_target_pairs={{0,8},{8,16},{16,24},{1,9},{9,17},{17,25},{2,10},{10,18},{18,26},{... | collective-permute-start | bytes 196616 | tf_op jit(solution)/shard_map/ppermute | solution.py:29
  191.3 7.0 %collective-permute-start.16 = (f32[1,1,64,128]{3,2,1,0:T(8,128)S(1)}, f32[1,1,64,128]{3,2,1,0:T(8,128)S(1)}, u32[]{:S(2)}, u32[]{:S(2)}) collective-permute-start(f32[1,1,64,128]{3,2,1,0:T(8,128)S(1)} %slice.728), channel_id=1, source_target_pairs={{8,0},{16,8},{24,16},{9,1},{17,9},{25,17},{10,2},{18,10},{26,18},{... | collective-permute-start | bytes 98312 | tf_op jit(solution)/shard_map/ppermute | solution.py:29
  199.2 7.4 %collective-permute-start.18 = (f32[1,1,64,128]{3,2,1,0:T(8,128)S(1)}, f32[1,1,64,128]{3,2,1,0:T(8,128)S(1)}, u32[]{:S(2)}, u32[]{:S(2)}) collective-permute-start(f32[1,1,64,128]{3,2,1,0:T(8,128)S(1)} %slice.732), channel_id=1, source_target_pairs={{0,8},{8,16},{16,24},{1,9},{9,17},{17,25},{2,10},{10,18},{18,26},{... | collective-permute-start | bytes 98312 | tf_op jit(solution)/shard_map/ppermute | solution.py:29
  252.9 7.0 %collective-permute-start.20 = (f32[1,1,64,128]{3,2,1,0:T(8,128)S(1)}, f32[1,1,64,128]{3,2,1,0:T(8,128)S(1)}, u32[]{:S(2)}, u32[]{:S(2)}) collective-permute-start(f32[1,1,64,128]{3,2,1,0:T(8,128)S(1)} %slice.738), channel_id=1, source_target_pairs={{8,0},{16,8},{24,16},{9,1},{17,9},{25,17},{10,2},{18,10},{26,18},{... | collective-permute-start | bytes 98312 | tf_op jit(solution)/shard_map/ppermute | solution.py:29
  254.2 5.7 %collective-permute-start.21 = (f32[1,32,1,128]{3,2,1,0:T(1,128)S(1)}, f32[1,32,1,128]{3,2,1,0:T(1,128)S(1)}, u32[]{:S(2)}, u32[]{:S(2)}) collective-permute-start(f32[1,32,1,128]{3,2,1,0:T(1,128)S(1)} %slice.740), channel_id=1, source_target_pairs={{1,0},{2,1},{3,2},{4,3},{5,4},{6,5},{7,6},{9,8},{10,9},{11,10},{12... | collective-permute-start | bytes 49160 | tf_op jit(solution)/shard_map/ppermute | solution.py:29
  260.8 9.0 %collective-permute-start.22 = (f32[1,1,64,128]{3,2,1,0:T(8,128)S(1)}, f32[1,1,64,128]{3,2,1,0:T(8,128)S(1)}, u32[]{:S(2)}, u32[]{:S(2)}) collective-permute-start(f32[1,1,64,128]{3,2,1,0:T(8,128)S(1)} %slice.742), channel_id=1, source_target_pairs={{0,8},{8,16},{16,24},{1,9},{9,17},{17,25},{2,10},{10,18},{18,26},{... | collective-permute-start | bytes 98312 | tf_op jit(solution)/shard_map/ppermute | solution.py:29
  325.2 5.9 %collective-permute-start.24 = (f32[2,1,64,128]{3,2,1,0:T(8,128)S(1)}, f32[2,1,64,128]{3,2,1,0:T(8,128)S(1)}, u32[]{:S(2)}, u32[]{:S(2)}) collective-permute-start(f32[2,1,64,128]{3,2,1,0:T(8,128)S(1)} %fusion.192), channel_id=1, source_target_pairs={{8,0},{16,8},{24,16},{9,1},{17,9},{25,17},{10,2},{18,10},{26,18},{... | collective-permute-start | bytes 196616 | tf_op jit(solution)/shard_map/ppermute | solution.py:29
  335.7 10.8 %collective-permute-start.26 = (f32[2,1,64,128]{3,2,1,0:T(8,128)S(1)}, f32[2,1,64,128]{3,2,1,0:T(8,128)S(1)}, u32[]{:S(2)}, u32[]{:S(2)}) collective-permute-start(f32[2,1,64,128]{3,2,1,0:T(8,128)S(1)} %pad_maximum_fusion.17), channel_id=1, source_target_pairs={{0,8},{8,16},{16,24},{1,9},{9,17},{17,25},{2,10},{10,18},{18,26},{... | collective-permute-start | bytes 196616 | tf_op jit(solution)/shard_map/ppermute | solution.py:29
  352.7 7.0 %collective-permute-start.28 = (f32[1,1,64,128]{3,2,1,0:T(8,128)S(1)}, f32[1,1,64,128]{3,2,1,0:T(8,128)S(1)}, u32[]{:S(2)}, u32[]{:S(2)}) collective-permute-start(f32[1,1,64,128]{3,2,1,0:T(8,128)S(1)} %slice.768), channel_id=1, source_target_pairs={{8,0},{16,8},{24,16},{9,1},{17,9},{25,17},{10,2},{18,10},{26,18},{... | collective-permute-start | bytes 98312 | tf_op jit(solution)/shard_map/ppermute | solution.py:29
  360.6 7.4 %collective-permute-start.30 = (f32[1,1,64,128]{3,2,1,0:T(8,128)S(1)}, f32[1,1,64,128]{3,2,1,0:T(8,128)S(1)}, u32[]{:S(2)}, u32[]{:S(2)}) collective-permute-start(f32[1,1,64,128]{3,2,1,0:T(8,128)S(1)} %slice.772), channel_id=1, source_target_pairs={{0,8},{8,16},{16,24},{1,9},{9,17},{17,25},{2,10},{10,18},{18,26},{... | collective-permute-start | bytes 98312 | tf_op jit(solution)/shard_map/ppermute | solution.py:29
  414.4 7.0 %collective-permute-start.32 = (f32[1,1,64,128]{3,2,1,0:T(8,128)S(1)}, f32[1,1,64,128]{3,2,1,0:T(8,128)S(1)}, u32[]{:S(2)}, u32[]{:S(2)}) collective-permute-start(f32[1,1,64,128]{3,2,1,0:T(8,128)S(1)} %slice.778), channel_id=1, source_target_pairs={{8,0},{16,8},{24,16},{9,1},{17,9},{25,17},{10,2},{18,10},{26,18},{... | collective-permute-start | bytes 98312 | tf_op jit(solution)/shard_map/ppermute | solution.py:29
  415.7 5.6 %collective-permute-start.33 = (f32[1,32,1,128]{3,2,1,0:T(1,128)S(1)}, f32[1,32,1,128]{3,2,1,0:T(1,128)S(1)}, u32[]{:S(2)}, u32[]{:S(2)}) collective-permute-start(f32[1,32,1,128]{3,2,1,0:T(1,128)S(1)} %slice.780), channel_id=1, source_target_pairs={{1,0},{2,1},{3,2},{4,3},{5,4},{6,5},{7,6},{9,8},{10,9},{11,10},{12... | collective-permute-start | bytes 49160 | tf_op jit(solution)/shard_map/ppermute | solution.py:29
  422.2 9.0 %collective-permute-start.34 = (f32[1,1,64,128]{3,2,1,0:T(8,128)S(1)}, f32[1,1,64,128]{3,2,1,0:T(8,128)S(1)}, u32[]{:S(2)}, u32[]{:S(2)}) collective-permute-start(f32[1,1,64,128]{3,2,1,0:T(8,128)S(1)} %slice.782), channel_id=1, source_target_pairs={{0,8},{8,16},{16,24},{1,9},{9,17},{17,25},{2,10},{10,18},{18,26},{... | collective-permute-start | bytes 98312 | tf_op jit(solution)/shard_map/ppermute | solution.py:29
  485.8 5.9 %collective-permute-start.36 = (f32[2,1,64,128]{3,2,1,0:T(8,128)S(1)}, f32[2,1,64,128]{3,2,1,0:T(8,128)S(1)}, u32[]{:S(2)}, u32[]{:S(2)}) collective-permute-start(f32[2,1,64,128]{3,2,1,0:T(8,128)S(1)} %fusion.191), channel_id=1, source_target_pairs={{8,0},{16,8},{24,16},{9,1},{17,9},{25,17},{10,2},{18,10},{26,18},{... | collective-permute-start | bytes 196616 | tf_op jit(solution)/shard_map/ppermute | solution.py:29
  496.0 9.6 %collective-permute-start.38 = (f32[2,1,64,128]{3,2,1,0:T(8,128)S(1)}, f32[2,1,64,128]{3,2,1,0:T(8,128)S(1)}, u32[]{:S(2)}, u32[]{:S(2)}) collective-permute-start(f32[2,1,64,128]{3,2,1,0:T(8,128)S(1)} %pad_maximum_fusion.16), channel_id=1, source_target_pairs={{0,8},{8,16},{16,24},{1,9},{9,17},{17,25},{2,10},{10,18},{18,26},{... | collective-permute-start | bytes 196616 | tf_op jit(solution)/shard_map/ppermute | solution.py:29
  (76 other events, 503.3 us)
where the time goes:
time: 522 us; the launch traced here: 512 us
  blocking collectives  236 us (45%)
  starting transfers between devices  120 us (23%)
  other arithmetic  94.5 us (18%)
  waiting for transfers between devices  30 us (6%)
  between operations  19.4 us (4%)
  local copies, waits for them, and re-layouts  11.2 us (2%)
    psum x6, blocking collectives, paired_products(): lax.psum((jnp.sum(residual * residual), jnp.sum(residual * image)), ('gx'...  236 us
    ppermute x40, starting transfers between devices, passed_along(): lax.ppermute(value, axis, [(source, source + steps) for source in range(l...  120 us
    ppermute x40, waiting for transfers between devices, passed_along(): lax.ppermute(value, axis, [(source, source + steps) for source in range(l...  30 us
    another operation x17, other arithmetic, apply_returned(): outgoing.append(jnp.stack(members))  27.2 us
    add x3, other arithmetic, apply_returned(): total = total + behind[1]  12.5 us
    sub x3, other arithmetic, local(): residual = residual - alpha * along  11.6 us
    reduce_sum x6, other arithmetic, paired_products(): jnp.sum(residual * image)  11.2 us
  transfers between devices with their start and end apart: 40, of which 23 were waited for; matrix products, arithmetic and copies ran while one was open for 3% of the time, Pallas kernels for 0%

commit v1 on v0

v1 whole, which is shorter than its diff:
```python
import functools

import jax
import jax.numpy as jnp
from jax import lax
from jax.experimental import pallas as pl
from jax.experimental.pallas import tpu as pltpu
from jax.sharding import PartitionSpec as P

explicit_table = (
    (0.0, 0.0, 0.0, 0.0),
    (0.5, 0.0, 0.0, 0.0),
    (0.25, 0.5, 0.0, 0.0),
    (0.2, 0.3, 0.5, 0.0),
)
implicit_table = (
    (0.0, 0.0, 0.0, 0.0),
    (0.25, 0.25, 0.0, 0.0),
    (0.25, 0.25, 0.25, 0.0),
    (0.15, 0.35, 0.25, 0.25),
)
section_weights = (0.15, 0.35, 0.25, 0.25)
implicit_diagonal = 0.25

MESH = pl.DeviceIdType.MESH
PAD = 8


def kernel(
    gx, gy, cot_hbm, speed_hbm, coeff_hbm, dirs_ref, out_ref,
    fields, mixes, cx, cy, cz, czm, px, py, pz, mx, my, mz, gdiag, fdiag,
    ysend, yrecv, landed, red_y, red_x, load_sem, send_sem, recv_sem, rys, ryr, rxs, rxr,
):
    nx, ny, nz = out_ref.shape
    me_x, me_y = lax.axis_index("gx"), lax.axis_index("gy")
    own = pl.ds(PAD, ny)
    up = pl.ds(PAD + 1, ny)
    down = pl.ds(PAD - 1, ny)
    lane = lax.broadcasted_iota(jnp.int32, (ny, nz), 1)
    last_lane = lane == nz - 1

    def ahead_z(v):
        return pltpu.roll(v, nz - 1, 1)

    def behind_z(v):
        return pltpu.roll(v, 1, 1)

    loads = [
        pltpu.make_async_copy(src, dst, load_sem.at[k])
        for k, (src, dst) in enumerate((
            (speed_hbm.at[0], mx.at[pl.ds(1, nx)]),
            (speed_hbm.at[1], my.at[:, own]),
            (speed_hbm.at[2], mz),
            (coeff_hbm.at[0], cx.at[pl.ds(1, nx)]),
            (coeff_hbm.at[1], cy.at[:, own]),
            (coeff_hbm.at[2], cz),
            (cot_hbm, fields.at[0, pl.ds(1, nx), own]),
        ))
    ]
    for load in loads:
        load.start()

    plane = jnp.zeros((ny, nz), jnp.float32)
    for k in range(7):
        fields[k, 0, own] = plane
        fields[k, nx + 1, own] = plane
    cx[0] = plane
    mx[0] = plane
    landed[0] = plane
    landed[1] = plane
    yrecv[...] = jnp.zeros_like(yrecv)

    def zero_rows(x, carry):
        cy[x, pl.ds(0, PAD)] = jnp.zeros((PAD, nz), jnp.float32)
        my[x, pl.ds(0, PAD)] = jnp.zeros((PAD, nz), jnp.float32)
        return carry

    lax.fori_loop(0, nx, zero_rows, 0)

    barrier = pltpu.get_barrier_semaphore()
    for off in range(1, gx):
        pl.semaphore_signal(barrier, inc=1, device_id={"gx": lax.rem(me_x + off, gx)}, device_id_type=MESH)
    for off in range(1, gy):
        pl.semaphore_signal(barrier, inc=1, device_id={"gy": lax.rem(me_y + off, gy)}, device_id_type=MESH)
    pl.semaphore_wait(barrier, gx + gy - 2)

    def x_down(tag, src, dst):
        return pltpu.make_async_remote_copy(
            src, dst, send_sem.at[tag, 0], recv_sem.at[tag, 0],
            device_id={"gx": lax.rem(me_x + gx - 1, gx)}, device_id_type=MESH)

    def x_up(tag, src, dst):
        return pltpu.make_async_remote_copy(
            src, dst, send_sem.at[tag, 1], recv_sem.at[tag, 1],
            device_id={"gx": lax.rem(me_x + 1, gx)}, device_id_type=MESH)

    def y_down(tag):
        return pltpu.make_async_remote_copy(
            ysend.at[tag, 0], yrecv.at[tag, 1], send_sem.at[tag, 2], recv_sem.at[tag, 2],
            device_id={"gy": lax.rem(me_y + gy - 1, gy)}, device_id_type=MESH)

    def y_up(tag):
        return pltpu.make_async_remote_copy(
            ysend.at[tag, 1], yrecv.at[tag, 0], send_sem.at[tag, 3], recv_sem.at[tag, 3],
            device_id={"gy": lax.rem(me_y + 1, gy)}, device_id_type=MESH)

    def copies(tag):
        field = fields.at[tag]
        return (
            x_down(tag, field.at[1, own], field.at[nx + 1, own]),
            x_up(tag, field.at[nx, own], field.at[0, own]),
            y_down(tag),
            y_up(tag),
        )

    not_low = (me_x > 0, me_y > 0)
    not_high = (me_x < gx - 1, me_y < gy - 1)

    def start(tag):
        xd, xu, yd, yu = copies(tag)
        pl.when(not_low[0])(xd.start)
        pl.when(not_high[0])(xu.start)
        pl.when(not_low[1])(yd.start)
        pl.when(not_high[1])(yu.start)

    def finish(tag):
        xd, xu, yd, yu = copies(tag)
        pl.when(not_high[0])(xd.wait_recv)
        pl.when(not_low[0])(xu.wait_recv)
        pl.when(not_high[1])(yd.wait_recv)
        pl.when(not_low[1])(yu.wait_recv)
        pl.when(not_low[0])(xd.wait_send)
        pl.when(not_high[0])(xu.wait_send)
        pl.when(not_low[1])(yd.wait_send)
        pl.when(not_high[1])(yu.wait_send)
        for x in range(nx):
            fields[tag, 1 + x, pl.ds(PAD - 1, 1)] = yrecv[tag, 0, pl.ds(x, 1)]
            fields[tag, 1 + x, pl.ds(PAD + ny, 1)] = yrecv[tag, 1, pl.ds(x, 1)]

    for load in loads:
        load.wait()

    dirs = [dirs_ref[d].astype(jnp.float32).T for d in range(3)]

    def prepare(x, carry):
        column = (lax.broadcasted_iota(jnp.int32, (nx, nz), 0) == x).astype(jnp.float32)
        upper = [
            jnp.dot(dirs[d], column, preferred_element_type=jnp.float32) > 0.5 for d in range(3)
        ]
        total = jnp.zeros((ny, nz), jnp.float32)
        s = mx[x + 1]
        total += mx[x]
        m = jnp.where(upper[0], s, 0.0)
        mx[x + 1] = m
        px[x] = s - m
        total += s - m
        s = my[x, own]
        m = jnp.where(upper[1], s, 0.0)
        my[x, own] = m
        py[x] = s - m
        total += s - m
        total += my[x, down]
        s = mz[x]
        m = jnp.where(upper[2], s, 0.0)
        p = s - m
        total += p
        m = jnp.where(last_lane, 0.0, m)
        total += behind_z(m)
        mz[x] = m
        pz[x] = jnp.where(last_lane, 0.0, p)
        fdiag[x] = total
        c = cz[x]
        m = jnp.where(last_lane, 0.0, c)
        czm[x] = m
        gdiag[x] = cx[x + 1] + cx[x] + cy[x, own] + cy[x, down] + c + behind_z(m)
        at = pl.ds(x, 1)
        ysend[0, 0, at] = fields[0, x + 1, pl.ds(PAD, 1)]
        ysend[0, 1, at] = fields[0, x + 1, pl.ds(PAD + ny - 1, 1)]
        ysend[7, 1, at] = cy[x, pl.ds(PAD + ny - 1, 1)]
        ysend[8, 1, at] = my[x, pl.ds(PAD + ny - 1, 1)]
        return carry

    lax.fori_loop(0, nx, prepare, 0)

    start(0)
    statics = (
        (x_up(7, cx.at[nx], landed.at[0]), y_up(7)),
        (x_up(8, mx.at[nx], landed.at[1]), y_up(8)),
    )
    for xu, yu in statics:
        pl.when(not_high[0])(xu.start)
        pl.when(not_high[1])(yu.start)
    for xu, yu in statics:
        pl.when(not_low[0])(xu.wait_recv)
        pl.when(not_low[1])(yu.wait_recv)
        pl.when(not_high[0])(xu.wait_send)
        pl.when(not_high[1])(yu.wait_send)
    finish(0)
    cx[0] = landed[0]
    mx[0] = landed[1]
    gdiag[0] += cx[0]
    fdiag[0] += mx[0]
    first = pl.ds(0, 1)
    for x in range(nx):
        row = yrecv[7, 0, pl.ds(x, 1)]
        cy[x, pl.ds(PAD - 1, 1)] = row
        gdiag[x, first] += row
        row = yrecv[8, 0, pl.ds(x, 1)]
        my[x, pl.ds(PAD - 1, 1)] = row
        fdiag[x, first] += row

    def spread(ref, x):
        v = ref[x + 1, own]
        total = cx[x + 1] * ref[x + 2, own] + cx[x] * ref[x, own]
        total += cy[x, own] * ref[x + 1, up] + cy[x, down] * ref[x + 1, down]
        c = czm[x]
        total += c * ahead_z(v) + behind_z(c * v)
        return v, total - gdiag[x] * v

    def carried(ref, x):
        v = ref[x + 1, own]
        total = px[x] * ref[x + 2, own] + mx[x] * ref[x, own]
        total += py[x] * ref[x + 1, up] + my[x, down] * ref[x + 1, down]
        total += pz[x] * ahead_z(v) + behind_z(mz[x] * v)
        return total - fdiag[x] * v

    def fold(v):
        return jnp.sum(v.reshape(ny // 8, 8, nz), axis=0)

    nothing = jnp.zeros((8, nz), jnp.float32)

    def keep(tag, x, v):
        fields[tag, x + 1, own] = v
        ysend[tag, 0, pl.ds(x, 1)] = v[:1]
        ysend[tag, 1, pl.ds(x, 1)] = v[ny - 1:]

    def reduced(step, sums):
        rows = [jnp.sum(s, axis=0, keepdims=True) for s in sums]
        red_y[step, me_y] = jnp.concatenate(rows + [jnp.zeros((4, nz), jnp.float32)], axis=0)

        def across(slots, axis, me, count, send, recv):
            out = [
                pltpu.make_async_remote_copy(
                    slots.at[step, me], slots.at[step, me], send.at[step, off], recv.at[step, me],
                    device_id={axis: lax.rem(me + off, count)}, device_id_type=MESH)
                for off in range(1, count)
            ]
            for copy in out:
                copy.start()
            for off in range(1, count):
                peer = lax.rem(me + off, count)
                pltpu.make_async_remote_copy(
                    slots.at[step, peer], slots.at[step, peer], send.at[step, off], recv.at[step, peer],
                    device_id={axis: peer}, device_id_type=MESH).wait_recv()
            total = slots[step, 0]
            for k in range(1, count):
                total = total + slots[step, k]
            for copy in out:
                copy.wait_send()
            return total

        red_x[step, me_x] = across(red_y, "gy", me_y, gy, rys, ryr)
        total = across(red_x, "gx", me_x, gx, rxs, rxr)
        total = jnp.broadcast_to(jnp.sum(total, axis=1, keepdims=True), (8, nz))
        return [total[k:k + 1] for k in range(4)]

    for step, section in enumerate((3, 2, 1, 0)):
        weight = section_weights[section]
        if step:
            def mix(x, carry):
                base = weight * fields[0, x]
                adv, dif = base, base
                for k in range(step):
                    later = 3 - k
                    nu = fields[4 + k, x]
                    adv = adv + explicit_table[later][section] * nu
                    dif = dif + implicit_table[later][section] * nu
                mixes[0, x] = adv
                mixes[1, x] = dif
                return carry

            lax.fori_loop(0, nx + 2, mix, 0)

        def source(x):
            if step == 0:
                field = fields.at[0]
                return weight * (spread(field, x)[1] + carried(field, x))
            return spread(mixes.at[1], x)[1] + carried(mixes.at[0], x)

        if section == 0:
            def last(x, carry):
                total = fields[0, x + 1, own] + source(x)
                for k in range(3):
                    total = total + fields[4 + k, x + 1, own]
                out_ref[x] = total
                return carry

            lax.fori_loop(0, nx, last, 0)
            break

        r_tag, w_tag = 1 + step, 4 + step

        def first_pass(x, m0):
            r = source(x)
            keep(r_tag, x, r)
            return m0 + fold(r * r)

        m0 = lax.fori_loop(0, nx, first_pass, nothing)
        start(r_tag)
        finish(r_tag)

        def second_pass(x, sums):
            m1, m2 = sums
            r, d = spread(fields.at[r_tag], x)
            w = r - implicit_diagonal * d
            keep(w_tag, x, w)
            return m1 + fold(r * w), m2 + fold(w * w)

        m1, m2 = lax.fori_loop(0, nx, second_pass, (nothing, nothing))
        start(w_tag)
        finish(w_tag)

        def third_pass(x, m3):
            ref = fields.at[w_tag]
            w = ref[x + 1, own]
            jump_x = ref[x + 2, own] - w
            jump_y = ref[x + 1, up] - w
            jump_z = jnp.where(last_lane, 0.0, ahead_z(w)) - w
            total = cx[x + 1] * jump_x * jump_x + cy[x, own] * jump_y * jump_y
            total += cz[x] * jump_z * jump_z
            return m3 + fold(implicit_diagonal * total)

        m3 = m2 + lax.fori_loop(0, nx, third_pass, nothing)
        m0, m1, m2, m3 = reduced(step, (m0, m1, m2, m3))
        alpha = m0 / m1
        rr = alpha * alpha * m2 - m0
        ratio = rr / m0
        product = m1 - 2.0 * alpha * m2 + alpha * alpha * m3
        alpha_next = rr / (product - ratio * rr / alpha)
        on_r = alpha + alpha_next * (1.0 + ratio)
        on_w = -alpha_next * alpha

        def combine(x, carry):
            fields[w_tag, x] = on_r * fields[r_tag, x] + on_w * fields[w_tag, x]
            return carry

        lax.fori_loop(0, nx + 2, combine, 0)


def local(gx, gy, cotangent, speed, coeff, dirs):
    nx, ny, nz = cotangent.shape
    f32 = jnp.float32
    rows = ny + 2 * PAD
    plain = pltpu.VMEM((nx, ny, nz), f32)
    dma = pltpu.SemaphoreType.DMA
    anywhere = pl.BlockSpec(memory_space=pl.ANY)
    return pl.pallas_call(
        functools.partial(kernel, gx, gy),
        out_shape=jax.ShapeDtypeStruct((nx, ny, nz), f32),
        in_specs=[anywhere, anywhere, anywhere, pl.BlockSpec(memory_space=pltpu.VMEM)],
        out_specs=pl.BlockSpec(memory_space=pltpu.VMEM),
        scratch_shapes=[
            pltpu.VMEM((7, nx + 2, rows, nz), f32),
            pltpu.VMEM((2, nx + 2, rows, nz), f32),
            pltpu.VMEM((nx + 1, ny, nz), f32),
            pltpu.VMEM((nx, rows, nz), f32),
            plain, plain,
            plain, plain, plain,
            pltpu.VMEM((nx + 1, ny, nz), f32),
            pltpu.VMEM((nx, rows, nz), f32),
            plain,
            plain, plain,
            pltpu.VMEM((9, 2, nx, nz), f32),
            pltpu.VMEM((9, 2, nx, nz), f32),
            pltpu.VMEM((2, ny, nz), f32),
            pltpu.VMEM((3, gy, 8, nz), f32),
            pltpu.VMEM((3, gx, 8, nz), f32),
            dma((7,)), dma((9, 4)), dma((9, 4)),
            dma((3, gy)), dma((3, gy)), dma((3, gx)), dma((3, gx)),
        ],
        compiler_params=pltpu.CompilerParams(
            collective_id=0, has_side_effects=True, vmem_limit_bytes=60 * 1024 * 1024
        ),
    )(cotangent, speed, coeff, dirs)


def solution(mesh):
    return jax.shard_map(
        functools.partial(local, mesh.shape["gx"], mesh.shape["gy"]),
        mesh=mesh,
        in_specs=(
            P("gx", "gy", None),
            P(None, "gx", "gy", None),
            P(None, "gx", "gy", None),
            P(None, "gx", "gy"),
        ),
        out_specs=P("gx", "gy", None),
        check_vma=False,
    )
```

time: 522 us -> 101 us (0.19)
  the two profiles are of different devices: /device:TPU:1 before, /device:TPU:0 now
where the time goes in v1:
time: 101 us
  Pallas kernels  98.2 us (97%)
  local copies, waits for them, and re-layouts  2.31 us (2%)
    pallas_call x1, Pallas kernels, local(): pl.pallas_call(functools.partial(kernel, gx, gy), out_shape=jax.ShapeDtyp...  98.2 us
    unnamed x1, local copies, waits for them, and re-layouts  2.31 us

profile of v1, /device:TPU:0, one launch (start us, length us, event | category | flops | bytes accessed | tf_op | source)
XLA Modules:
  0.0 100.5 jit_solution(6565766326453177140)
XLA Ops:
  0.0 98.2 %shard_map.46 = f32[32,64,128]{2,1,0:T(8,128)} custom-call(f32[32,64,128]{2,1,0:T(8,128)} %cot_hbm.1, f32[3,32,64,128]{3,2,1,0:T(8,128)} %speed_hbm.1, f32[3,32,64,128]{3,2,1,0:T(8,128)} %coeff_hbm.1, s32[3,32,64]{2,1,0:T(8,128)} %dirs_ref.1), custom_call_target="tpu_custom_call" | custom-call | tf_op jit(solution)/shard_map/pallas_call | solution.py:357
  98.2 2.3 %copy.6 = f32[32,64,128]{2,1,0:T(8,128)} copy(f32[32,64,128]{2,1,0:T(8,128)} %shard_map.46) | data formatting | bytes 2097152

commit v2 on v1

v2 whole, which is shorter than its diff:
```python
import functools

import jax
import jax.numpy as jnp
from jax import lax
from jax.experimental import pallas as pl
from jax.experimental.pallas import tpu as pltpu
from jax.sharding import PartitionSpec as P

explicit_table = (
    (0.0, 0.0, 0.0, 0.0),
    (0.5, 0.0, 0.0, 0.0),
    (0.25, 0.5, 0.0, 0.0),
    (0.2, 0.3, 0.5, 0.0),
)
implicit_table = (
    (0.0, 0.0, 0.0, 0.0),
    (0.25, 0.25, 0.0, 0.0),
    (0.25, 0.25, 0.25, 0.0),
    (0.15, 0.35, 0.25, 0.25),
)
section_weights = (0.15, 0.35, 0.25, 0.25)
implicit_diagonal = 0.25

MESH = pl.DeviceIdType.MESH
PAD = 8


def kernel(
    gx, gy, cot_hbm, speed_hbm, coeff_hbm, dirs_ref, out_ref,
    fields, fr, fw, dw, base, cx, cy, cz, czm, px, py, pz, mx, my, mz, gdiag, fdiag,
    ysend, yrecv, landed, stage, red_y, red_x, load_sem, send_sem, recv_sem, rys, ryr, rxs, rxr,
):
    nx, ny, nz = out_ref.shape
    me_x, me_y = lax.axis_index("gx"), lax.axis_index("gy")
    own = pl.ds(PAD, ny)
    up = pl.ds(PAD + 1, ny)
    down = pl.ds(PAD - 1, ny)
    lane = lax.broadcasted_iota(jnp.int32, (ny, nz), 1)
    last_lane = lane == nz - 1

    def ahead_z(v):
        return pltpu.roll(v, nz - 1, 1)

    def behind_z(v):
        return pltpu.roll(v, 1, 1)

    loads = [
        pltpu.make_async_copy(src, dst, load_sem.at[k])
        for k, (src, dst) in enumerate((
            (speed_hbm.at[0], mx.at[pl.ds(1, nx)]),
            (speed_hbm.at[1], my.at[:, own]),
            (speed_hbm.at[2], mz),
            (coeff_hbm.at[0], cx.at[pl.ds(1, nx)]),
            (coeff_hbm.at[1], cy.at[:, own]),
            (coeff_hbm.at[2], cz),
            (cot_hbm, fields.at[0, pl.ds(1, nx), own]),
        ))
    ]
    for load in loads:
        load.start()

    plane = jnp.zeros((ny, nz), jnp.float32)
    for k in range(7):
        fields[k, 0, own] = plane
        fields[k, nx + 1, own] = plane
    cx[0] = plane
    mx[0] = plane
    landed[0] = plane
    landed[1] = plane
    yrecv[...] = jnp.zeros_like(yrecv)

    def zero_rows(x, carry):
        cy[x, pl.ds(0, PAD)] = jnp.zeros((PAD, nz), jnp.float32)
        my[x, pl.ds(0, PAD)] = jnp.zeros((PAD, nz), jnp.float32)
        for k in range(1, 7):
            fields[k, x + 1, pl.ds(0, PAD)] = jnp.zeros((PAD, nz), jnp.float32)
            fields[k, x + 1, pl.ds(PAD + ny, PAD)] = jnp.zeros((PAD, nz), jnp.float32)
        return carry

    lax.fori_loop(0, nx, zero_rows, 0)

    barrier = pltpu.get_barrier_semaphore()
    for off in range(1, gx):
        pl.semaphore_signal(barrier, inc=1, device_id={"gx": lax.rem(me_x + off, gx)}, device_id_type=MESH)
    for off in range(1, gy):
        pl.semaphore_signal(barrier, inc=1, device_id={"gy": lax.rem(me_y + off, gy)}, device_id_type=MESH)
    pl.semaphore_wait(barrier, gx + gy - 2)

    def x_down(tag, src, dst):
        return pltpu.make_async_remote_copy(
            src, dst, send_sem.at[tag, 0], recv_sem.at[tag, 0],
            device_id={"gx": lax.rem(me_x + gx - 1, gx)}, device_id_type=MESH)

    def x_up(tag, src, dst):
        return pltpu.make_async_remote_copy(
            src, dst, send_sem.at[tag, 1], recv_sem.at[tag, 1],
            device_id={"gx": lax.rem(me_x + 1, gx)}, device_id_type=MESH)

    def y_down(tag):
        return pltpu.make_async_remote_copy(
            ysend.at[tag, 0], yrecv.at[tag, 1], send_sem.at[tag, 2], recv_sem.at[tag, 2],
            device_id={"gy": lax.rem(me_y + gy - 1, gy)}, device_id_type=MESH)

    def y_up(tag):
        return pltpu.make_async_remote_copy(
            ysend.at[tag, 1], yrecv.at[tag, 0], send_sem.at[tag, 3], recv_sem.at[tag, 3],
            device_id={"gy": lax.rem(me_y + 1, gy)}, device_id_type=MESH)

    def copies(tag):
        field = fields.at[tag]
        return (
            x_down(tag, field.at[1, own], field.at[nx + 1, own]),
            x_up(tag, field.at[nx, own], field.at[0, own]),
            y_down(tag),
            y_up(tag),
        )

    low_x, low_y = me_x > 0, me_y > 0
    high_x, high_y = me_x < gx - 1, me_y < gy - 1

    def start_x(tag):
        xd, xu, _, _ = copies(tag)
        pl.when(low_x)(xd.start)
        pl.when(high_x)(xu.start)

    def start_y(tag):
        _, _, yd, yu = copies(tag)
        pl.when(low_y)(yd.start)
        pl.when(high_y)(yu.start)

    def arrive(tag):
        xd, xu, yd, yu = copies(tag)
        pl.when(high_y)(yd.wait_recv)
        pl.when(low_y)(yu.wait_recv)
        pl.when(high_x)(xd.wait_recv)
        pl.when(low_x)(xu.wait_recv)

    def sent(tag):
        xd, xu, yd, yu = copies(tag)
        pl.when(low_x)(xd.wait_send)
        pl.when(high_x)(xu.wait_send)
        pl.when(low_y)(yd.wait_send)
        pl.when(high_y)(yu.wait_send)

    def unpack(tag):
        for x in range(nx):
            fields[tag, 1 + x, pl.ds(PAD - 1, 1)] = yrecv[tag, 0, pl.ds(x, 1)]
            fields[tag, 1 + x, pl.ds(PAD + ny, 1)] = yrecv[tag, 1, pl.ds(x, 1)]

    for load in loads:
        load.wait()

    for x in range(nx):
        at = pl.ds(x, 1)
        ysend[0, 0, at] = fields[0, x + 1, pl.ds(PAD, 1)]
        ysend[0, 1, at] = fields[0, x + 1, pl.ds(PAD + ny - 1, 1)]
        ysend[7, 1, at] = cy[x, pl.ds(PAD + ny - 1, 1)]
        ysend[8, 1, at] = my[x, pl.ds(PAD + ny - 1, 1)]
    dirs = [dirs_ref[d].astype(jnp.float32).T for d in range(3)]
    edge = jnp.broadcast_to(dirs_ref[1][:, ny - 1:], (nx, nz))
    ysend[8, 1] = jnp.where(edge > 0, ysend[8, 1], 0.0)

    def upper(d, x):
        column = (lax.broadcasted_iota(jnp.int32, (nx, nz), 0) == x).astype(jnp.float32)
        return jnp.dot(dirs[d], column, preferred_element_type=jnp.float32) > 0.5

    stage[...] = jnp.where(upper(0, nx - 1), mx[nx], 0.0)
    start_x(0)
    start_y(0)
    statics = (
        (x_up(7, cx.at[nx], landed.at[0]), y_up(7)),
        (x_up(8, stage, landed.at[1]), y_up(8)),
    )
    for xu, yu in statics:
        pl.when(high_x)(xu.start)
        pl.when(high_y)(yu.start)

    def prepare(x, carry):
        total = mx[x]
        s = mx[x + 1]
        m = jnp.where(upper(0, x), s, 0.0)
        mx[x + 1] = m
        px[x] = s - m
        total += s - m
        s = my[x, own]
        m = jnp.where(upper(1, x), s, 0.0)
        my[x, own] = m
        py[x] = s - m
        total += s - m
        total += my[x, down]
        s = mz[x]
        m = jnp.where(upper(2, x), s, 0.0)
        p = s - m
        total += p
        m = jnp.where(last_lane, 0.0, m)
        total += behind_z(m)
        mz[x] = m
        pz[x] = jnp.where(last_lane, 0.0, p)
        fdiag[x] = total
        c = cz[x]
        m = jnp.where(last_lane, 0.0, c)
        czm[x] = m
        gdiag[x] = cx[x + 1] + cx[x] + cy[x, own] + cy[x, down] + c + behind_z(m)
        return carry

    lax.fori_loop(0, nx, prepare, 0)

    arrive(0)
    for xu, yu in statics:
        pl.when(low_x)(xu.wait_recv)
        pl.when(low_y)(yu.wait_recv)
    unpack(0)
    cx[0] = landed[0]
    mx[0] = landed[1]
    gdiag[0] += cx[0]
    fdiag[0] += mx[0]
    first = pl.ds(0, 1)
    for x in range(nx):
        row = yrecv[7, 0, pl.ds(x, 1)]
        cy[x, pl.ds(PAD - 1, 1)] = row
        gdiag[x, first] += row
        row = yrecv[8, 0, pl.ds(x, 1)]
        my[x, pl.ds(PAD - 1, 1)] = row
        fdiag[x, first] += row

    def spread(ref, x):
        v = ref[x + 1, own]
        total = cx[x + 1] * ref[x + 2, own] + cx[x] * ref[x, own]
        total += cy[x, own] * ref[x + 1, up] + cy[x, down] * ref[x + 1, down]
        c = czm[x]
        total += c * ahead_z(v) + behind_z(c * v)
        return v, total - gdiag[x] * v

    def carried(ref, x):
        v = ref[x + 1, own]
        total = px[x] * ref[x + 2, own] + mx[x] * ref[x, own]
        total += py[x] * ref[x + 1, up] + my[x, down] * ref[x + 1, down]
        total += pz[x] * ahead_z(v) + behind_z(mz[x] * v)
        return total - fdiag[x] * v

    def fold(v):
        return jnp.sum(v.reshape(v.shape[0] // 8, 8, nz), axis=0)

    nothing = jnp.zeros((8, nz), jnp.float32)

    def keep(tag, x, v):
        fields[tag, x + 1, own] = v
        ysend[tag, 0, pl.ds(x, 1)] = v[:1]
        ysend[tag, 1, pl.ds(x, 1)] = v[ny - 1:]

    def across(step, slots, axis, me, count, send, recv):
        out = [
            pltpu.make_async_remote_copy(
                slots.at[step, me], slots.at[step, me], send.at[step, off], recv.at[step, me],
                device_id={axis: lax.rem(me + off, count)}, device_id_type=MESH)
            for off in range(1, count)
        ]
        for copy in out:
            copy.start()

        def result():
            for off in range(1, count):
                peer = lax.rem(me + off, count)
                pltpu.make_async_remote_copy(
                    slots.at[step, peer], slots.at[step, peer], send.at[step, off], recv.at[step, peer],
                    device_id={axis: peer}, device_id_type=MESH).wait_recv()
            total = slots[step, 0]
            for k in range(1, count):
                total = total + slots[step, k]
            return total

        return out, result

    row_x = lax.broadcasted_iota(jnp.int32, (nx, nz), 0)
    between = jnp.logical_and(row_x > 0, row_x < nx - 1)
    pending = []
    for step, section in enumerate((3, 2, 1)):
        r_tag, w_tag = 1 + step, 4 + step
        r_ref, w_ref = fields.at[r_tag], fields.at[w_tag]

        def first_pass(x, m0):
            if step == 0:
                c_ref = fields.at[0]
                r = section_weights[3] * (spread(c_ref, x)[1] + carried(c_ref, x))
            else:
                r = following(x)
            keep(r_tag, x, r)
            return m0 + fold(r * r)

        m0 = first_pass(nx - 1, first_pass(0, nothing))
        start_x(r_tag)
        m0 = lax.fori_loop(1, nx - 1, first_pass, m0)
        start_y(r_tag)

        def second_pass(x, sums):
            m1, m2 = sums
            r, d = spread(r_ref, x)
            w = r - implicit_diagonal * d
            keep(w_tag, x, w)
            return m1 + fold(r * w), m2 + fold(w * w)

        sums = lax.fori_loop(1, nx - 1, second_pass, (nothing, nothing))
        arrive(r_tag)
        unpack(r_tag)
        m1, m2 = second_pass(nx - 1, second_pass(0, sums))
        start_x(w_tag)
        for side, face in ((0, yrecv[7, 0]), (1, ysend[7, 1])):
            change = jnp.where(between, -implicit_diagonal * face * yrecv[r_tag, side], 0.0)
            w = ysend[w_tag, side]
            ysend[w_tag, side] = w + change
            m1 += fold(ysend[r_tag, side] * change)
            m2 += fold((2.0 * w + change) * change)
        start_y(w_tag)
        for x in range(1, nx - 1):
            fields[w_tag, 1 + x, pl.ds(PAD, 1)] = ysend[w_tag, 0, pl.ds(x, 1)]
            fields[w_tag, 1 + x, pl.ds(PAD + ny - 1, 1)] = ysend[w_tag, 1, pl.ds(x, 1)]

        def third_pass(x, m3):
            w = w_ref[x + 1, own]
            jump_x = w_ref[x + 2, own] - w
            jump_y = w_ref[x + 1, up] - w
            jump_z = jnp.where(last_lane, 0.0, ahead_z(w)) - w
            total = cx[x + 1] * jump_x * jump_x + cy[x, own] * jump_y * jump_y
            total += cz[x] * jump_z * jump_z
            return m3 + fold(total)

        m3 = lax.fori_loop(0, nx - 1, third_pass, nothing)

        def carry_r(x, carry):
            fr[step, x] = carried(r_ref, x)
            return carry

        lax.fori_loop(0, nx, carry_r, 0)
        arrive(w_tag)
        m3 = third_pass(nx - 1, m3)
        above = yrecv[w_tag, 1]
        m3 += fold(ysend[7, 1] * above * (above - 2.0 * ysend[w_tag, 1]))
        m3 = m2 + implicit_diagonal * m3
        rows = [jnp.sum(m, axis=0, keepdims=True) for m in (m0, m1, m2, m3)]
        red_y[step, me_y] = jnp.concatenate(rows + [jnp.zeros((4, nz), jnp.float32)], axis=0)
        out, result = across(step, red_y, "gy", me_y, gy, rys, ryr)
        pending += out
        unpack(w_tag)

        def carry_w(x, carry):
            fw[step, x] = carried(w_ref, x)
            dw[step, x] = spread(w_ref, x)[1]
            return carry

        lax.fori_loop(0, nx, carry_w, 0)
        red_x[step, me_x] = result()
        out, result = across(step, red_x, "gx", me_x, gx, rxs, rxr)
        pending += out

        target = section - 1
        share = section_weights[target] / section_weights[3]

        def gather(x, carry):
            total = share * fields[1, x + 1, own]
            for k in range(step):
                total += explicit_table[3 - k][target] * fr[k, x] + implicit_table[3 - k][target] * dw[k, x]
            if target == 0:
                total += fields[0, x + 1, own]
                for k in range(step):
                    on_r, on_w = weights[k]
                    total += on_r * fields[1 + k, x + 1, own] + on_w * fields[4 + k, x + 1, own]
            base[x] = total
            return carry

        if step == 0:
            weights = []
        lax.fori_loop(0, nx, gather, 0)

        total = result()
        total = jnp.broadcast_to(jnp.sum(total, axis=1, keepdims=True), (8, nz))
        m0, m1, m2, m3 = [total[k:k + 1] for k in range(4)]
        alpha = m0 / m1
        rr = alpha * alpha * m2 - m0
        ratio = rr / m0
        product = m1 - 2.0 * alpha * m2 + alpha * alpha * m3
        alpha_next = rr / (product - ratio * rr / alpha)
        on_r = alpha + alpha_next * (1.0 + ratio)
        on_w = -alpha_next * alpha
        weights.append((on_r, on_w))

        def following(x, step=step, section=section, target=target, on_r=on_r, on_w=on_w):
            r, w = fields[1 + step, x + 1, own], fields[4 + step, x + 1, own]
            advected = on_r * fr[step, x] + on_w * fw[step, x]
            diffused = (on_r / implicit_diagonal) * (r - w) + on_w * dw[step, x]
            total = base[x]
            total += explicit_table[section][target] * advected
            total += implicit_table[section][target] * diffused
            if target == 0:
                return total + on_r * r + on_w * w
            fr[step, x] = advected
            dw[step, x] = diffused
            return total

    def last(x, carry):
        out_ref[x] = following(x)
        return carry

    lax.fori_loop(0, nx, last, 0)
    for xu, yu in statics:
        pl.when(high_x)(xu.wait_send)
        pl.when(high_y)(yu.wait_send)
    for tag in range(7):
        sent(tag)
    for copy in pending:
        copy.wait_send()


def local(gx, gy, cotangent, speed, coeff, dirs):
    nx, ny, nz = cotangent.shape
    f32 = jnp.float32
    rows = ny + 2 * PAD
    plain = pltpu.VMEM((nx, ny, nz), f32)
    dma = pltpu.SemaphoreType.DMA
    anywhere = pl.BlockSpec(memory_space=pl.ANY)
    return pl.pallas_call(
        functools.partial(kernel, gx, gy),
        out_shape=jax.ShapeDtypeStruct((nx, ny, nz), f32),
        in_specs=[anywhere, anywhere, anywhere, pl.BlockSpec(memory_space=pltpu.VMEM)],
        out_specs=pl.BlockSpec(memory_space=pltpu.VMEM),
        scratch_shapes=[
            pltpu.VMEM((7, nx + 2, rows, nz), f32),
            pltpu.VMEM((3, nx, ny, nz), f32),
            pltpu.VMEM((3, nx, ny, nz), f32),
            pltpu.VMEM((3, nx, ny, nz), f32),
            plain,
            pltpu.VMEM((nx + 1, ny, nz), f32),
            pltpu.VMEM((nx, rows, nz), f32),
            plain, plain,
            plain, plain, plain,
            pltpu.VMEM((nx + 1, ny, nz), f32),
            pltpu.VMEM((nx, rows, nz), f32),
            plain,
            plain, plain,
            pltpu.VMEM((9, 2, nx, nz), f32),
            pltpu.VMEM((9, 2, nx, nz), f32),
            pltpu.VMEM((2, ny, nz), f32),
            pltpu.VMEM((ny, nz), f32),
            pltpu.VMEM((3, gy, 8, nz), f32),
            pltpu.VMEM((3, gx, 8, nz), f32),
            dma((7,)), dma((9, 4)), dma((9, 4)),
            dma((3, gy)), dma((3, gy)), dma((3, gx)), dma((3, gx)),
        ],
        compiler_params=pltpu.CompilerParams(
            collective_id=0, has_side_effects=True, vmem_limit_bytes=60 * 1024 * 1024
        ),
    )(cotangent, speed, coeff, dirs)


def solution(mesh):
    return jax.shard_map(
        functools.partial(local, mesh.shape["gx"], mesh.shape["gy"]),
        mesh=mesh,
        in_specs=(
            P("gx", "gy", None),
            P(None, "gx", "gy", None),
            P(None, "gx", "gy", None),
            P(None, "gx", "gy"),
        ),
        out_specs=P("gx", "gy", None),
        check_vma=False,
    )
```

time: 101 us -> 72.4 us (0.72)
  Pallas kernels: 98.2 us -> 69.9 us
    pallas_call x1, Pallas kernels: 98.2 us -> 69.9 us  [local(): pl.pallas_call(functools.partial(kernel, gx, gy), out_shape=jax.ShapeDtyp...]
where the time goes in v2:
time: 72.4 us; the launch traced here: 72.2 us
  Pallas kernels  69.9 us (97%)
  local copies, waits for them, and re-layouts  2.31 us (3%)
    pallas_call x1, Pallas kernels, local(): pl.pallas_call(functools.partial(kernel, gx, gy), out_shape=jax.ShapeDtyp...  69.9 us
    unnamed x1, local copies, waits for them, and re-layouts  2.31 us

profile of v2, /device:TPU:0, one launch (start us, length us, event | category | flops | bytes accessed | tf_op | source)
XLA Modules:
  0.0 72.2 jit_solution(5782452118801514301)
XLA Ops:
  0.0 69.9 %shard_map.46 = f32[32,64,128]{2,1,0:T(8,128)} custom-call(f32[32,64,128]{2,1,0:T(8,128)} %cot_hbm.1, f32[3,32,64,128]{3,2,1,0:T(8,128)} %speed_hbm.1, f32[3,32,64,128]{3,2,1,0:T(8,128)} %coeff_hbm.1, s32[3,32,64]{2,1,0:T(8,128)} %dirs_ref.1), custom_call_target="tpu_custom_call" | custom-call | tf_op jit(solution)/shard_map/pallas_call | solution.py:421
  69.9 2.3 %copy.6 = f32[32,64,128]{2,1,0:T(8,128)} copy(f32[32,64,128]{2,1,0:T(8,128)} %shard_map.46) | data formatting | bytes 2097152

commit v3 on v2

--- a/solution.py
+++ b/solution.py
@@ -26,12 +26,36 @@
 PAD = 8
 
 
+GROUP = {"masks": 4, "diagonals": 2, "source": 2, "next": 2, "image": 2, "energy": 4, "carry": 4, "both": 2, "gather": 2}
+
+
+def grouped(name, low, high, value, store, carry):
+    size = GROUP[name]
+
+    def group(planes, carry):
+        found = []
+        for x in planes:
+            carry, kept = value(x, carry)
+            found.append(kept)
+        for x, kept in zip(planes, found):
+            store(x, kept)
+        return carry
+
+    turns = (high - low) // size
+    carry = lax.fori_loop(
+        0, turns, lambda t, c: group([low + t * size + k for k in range(size)], c), carry)
+    rest = list(range(low + turns * size, high))
+    return group(rest, carry) if rest else carry
+
+
 def kernel(
     gx, gy, cot_hbm, speed_hbm, coeff_hbm, dirs_ref, out_ref,
-    fields, fr, fw, dw, base, cx, cy, cz, czm, px, py, pz, mx, my, mz, gdiag, fdiag,
+    f0, f1, f2, f3, f4, f5, f6, fr0, fr1, fr2, fw0, fw1, fw2, dw0, dw1, dw2, base, cx, cy, cz, czm, px, py, pz, mx, my, mz, gdiag, fdiag,
     ysend, yrecv, landed, stage, red_y, red_x, load_sem, send_sem, recv_sem, rys, ryr, rxs, rxr,
 ):
     nx, ny, nz = out_ref.shape
+    fields = (f0, f1, f2, f3, f4, f5, f6)
+    fr, fw, dw = (fr0, fr1, fr2), (fw0, fw1, fw2), (dw0, dw1, dw2)
     me_x, me_y = lax.axis_index("gx"), lax.axis_index("gy")
     own = pl.ds(PAD, ny)
     up = pl.ds(PAD + 1, ny)
@@ -48,13 +72,13 @@
     loads = [
         pltpu.make_async_copy(src, dst, load_sem.at[k])
         for k, (src, dst) in enumerate((
-            (speed_hbm.at[0], mx.at[pl.ds(1, nx)]),
-            (speed_hbm.at[1], my.at[:, own]),
-            (speed_hbm.at[2], mz),
+            (speed_hbm.at[0], px),
+            (speed_hbm.at[1], py),
+            (speed_hbm.at[2], pz),
             (coeff_hbm.at[0], cx.at[pl.ds(1, nx)]),
             (coeff_hbm.at[1], cy.at[:, own]),
             (coeff_hbm.at[2], cz),
-            (cot_hbm, fields.at[0, pl.ds(1, nx), own]),
+            (cot_hbm, fields[0].at[pl.ds(1, nx), own]),
         ))
     ]
     for load in loads:
@@ -62,8 +86,8 @@
 
     plane = jnp.zeros((ny, nz), jnp.float32)
     for k in range(7):
-        fields[k, 0, own] = plane
-        fields[k, nx + 1, own] = plane
+        fields[k][0, own] = plane
+        fields[k][nx + 1, own] = plane
     cx[0] = plane
     mx[0] = plane
     landed[0] = plane
@@ -74,8 +98,8 @@
         cy[x, pl.ds(0, PAD)] = jnp.zeros((PAD, nz), jnp.float32)
         my[x, pl.ds(0, PAD)] = jnp.zeros((PAD, nz), jnp.float32)
         for k in range(1, 7):
-            fields[k, x + 1, pl.ds(0, PAD)] = jnp.zeros((PAD, nz), jnp.float32)
-            fields[k, x + 1, pl.ds(PAD + ny, PAD)] = jnp.zeros((PAD, nz), jnp.float32)
+            fields[k][x + 1, pl.ds(0, PAD)] = jnp.zeros((PAD, nz), jnp.float32)
+            fields[k][x + 1, pl.ds(PAD + ny, PAD)] = jnp.zeros((PAD, nz), jnp.float32)
         return carry
 
     lax.fori_loop(0, nx, zero_rows, 0)
@@ -108,7 +132,7 @@
             device_id={"gy": lax.rem(me_y + 1, gy)}, device_id_type=MESH)
 
     def copies(tag):
-        field = fields.at[tag]
+        field = fields[tag]
         return (
             x_down(tag, field.at[1, own], field.at[nx + 1, own]),
             x_up(tag, field.at[nx, own], field.at[0, own]),
@@ -145,18 +169,18 @@
 
     def unpack(tag):
         for x in range(nx):
-            fields[tag, 1 + x, pl.ds(PAD - 1, 1)] = yrecv[tag, 0, pl.ds(x, 1)]
-            fields[tag, 1 + x, pl.ds(PAD + ny, 1)] = yrecv[tag, 1, pl.ds(x, 1)]
+            fields[tag][1 + x, pl.ds(PAD - 1, 1)] = yrecv[tag, 0, pl.ds(x, 1)]
+            fields[tag][1 + x, pl.ds(PAD + ny, 1)] = yrecv[tag, 1, pl.ds(x, 1)]
 
     for load in loads:
         load.wait()
 
     for x in range(nx):
         at = pl.ds(x, 1)
-        ysend[0, 0, at] = fields[0, x + 1, pl.ds(PAD, 1)]
-        ysend[0, 1, at] = fields[0, x + 1, pl.ds(PAD + ny - 1, 1)]
+        ysend[0, 0, at] = fields[0][x + 1, pl.ds(PAD, 1)]
+        ysend[0, 1, at] = fields[0][x + 1, pl.ds(PAD + ny - 1, 1)]
         ysend[7, 1, at] = cy[x, pl.ds(PAD + ny - 1, 1)]
-        ysend[8, 1, at] = my[x, pl.ds(PAD + ny - 1, 1)]
+        ysend[8, 1, at] = py[x, pl.ds(ny - 1, 1)]
     dirs = [dirs_ref[d].astype(jnp.float32).T for d in range(3)]
     edge = jnp.broadcast_to(dirs_ref[1][:, ny - 1:], (nx, nz))
     ysend[8, 1] = jnp.where(edge > 0, ysend[8, 1], 0.0)
@@ -165,7 +189,7 @@
         column = (lax.broadcasted_iota(jnp.int32, (nx, nz), 0) == x).astype(jnp.float32)
         return jnp.dot(dirs[d], column, preferred_element_type=jnp.float32) > 0.5
 
-    stage[...] = jnp.where(upper(0, nx - 1), mx[nx], 0.0)
+    stage[...] = jnp.where(upper(0, nx - 1), px[nx - 1], 0.0)
     start_x(0)
     start_y(0)
     statics = (
@@ -176,35 +200,31 @@
         pl.when(high_x)(xu.start)
         pl.when(high_y)(yu.start)
 
-    def prepare(x, carry):
-        total = mx[x]
-        s = mx[x + 1]
-        m = jnp.where(upper(0, x), s, 0.0)
-        mx[x + 1] = m
-        px[x] = s - m
-        total += s - m
-        s = my[x, own]
-        m = jnp.where(upper(1, x), s, 0.0)
-        my[x, own] = m
-        py[x] = s - m
-        total += s - m
-        total += my[x, down]
-        s = mz[x]
-        m = jnp.where(upper(2, x), s, 0.0)
-        p = s - m
-        total += p
-        m = jnp.where(last_lane, 0.0, m)
-        total += behind_z(m)
-        mz[x] = m
-        pz[x] = jnp.where(last_lane, 0.0, p)
-        fdiag[x] = total
-        c = cz[x]
-        m = jnp.where(last_lane, 0.0, c)
-        czm[x] = m
-        gdiag[x] = cx[x + 1] + cx[x] + cy[x, own] + cy[x, down] + c + behind_z(m)
-        return carry
-
-    lax.fori_loop(0, nx, prepare, 0)
+    def masks(x, carry):
+        low = [jnp.where(upper(d, x), ref[x], 0.0) for d, ref in enumerate((px, py, pz))]
+        return carry, (low, [ref[x] - m for m, ref in zip(low, (px, py, pz))], cz[x])
+
+    def store_masks(x, kept):
+        low, high, c = kept
+        mx[x + 1] = low[0]
+        my[x, own] = low[1]
+        mz[x] = jnp.where(last_lane, 0.0, low[2])
+        px[x], py[x] = high[0], high[1]
+        pz[x] = high[2]
+        czm[x] = jnp.where(last_lane, 0.0, c)
+
+    grouped("masks", 0, nx, masks, store_masks, 0)
+
+    def diagonals(x, carry):
+        p = pz[x]
+        f = px[x] + mx[x] + py[x] + my[x, down] + p + behind_z(mz[x])
+        g = cx[x + 1] + cx[x] + cy[x, own] + cy[x, down] + cz[x] + behind_z(czm[x])
+        return carry, (f, g, jnp.where(last_lane, 0.0, p))
+
+    def store_diagonals(x, kept):
+        fdiag[x], gdiag[x], pz[x] = kept
+
+    grouped("diagonals", 0, nx, diagonals, store_diagonals, 0)
 
     arrive(0)
     for xu, yu in statics:
@@ -245,7 +265,7 @@
     nothing = jnp.zeros((8, nz), jnp.float32)
 
     def keep(tag, x, v):
-        fields[tag, x + 1, own] = v
+        fields[tag][x + 1, own] = v
         ysend[tag, 0, pl.ds(x, 1)] = v[:1]
         ysend[tag, 1, pl.ds(x, 1)] = v[ny - 1:]
 
@@ -277,33 +297,47 @@
     pending = []
     for step, section in enumerate((3, 2, 1)):
         r_tag, w_tag = 1 + step, 4 + step
-        r_ref, w_ref = fields.at[r_tag], fields.at[w_tag]
+        r_ref, w_ref = fields[r_tag], fields[w_tag]
 
         def first_pass(x, m0):
             if step == 0:
-                c_ref = fields.at[0]
+                c_ref = fields[0]
                 r = section_weights[3] * (spread(c_ref, x)[1] + carried(c_ref, x))
             else:
                 r = following(x)
+            r, more = r if step else (r, None)
+            return m0 + fold(r * r), (r, more)
+
+        def store_first(x, kept):
+            r, more = kept
             keep(r_tag, x, r)
-            return m0 + fold(r * r)
-
-        m0 = first_pass(nx - 1, first_pass(0, nothing))
+            if more is not None:
+                fr[step - 1][x], dw[step - 1][x] = more
+
+        m0 = nothing
+        for x in (0, nx - 1):
+            m0, kept = first_pass(x, m0)
+            store_first(x, kept)
         start_x(r_tag)
-        m0 = lax.fori_loop(1, nx - 1, first_pass, m0)
+        m0 = grouped("next" if step else "source", 1, nx - 1, first_pass, store_first, m0)
         start_y(r_tag)
 
         def second_pass(x, sums):
             m1, m2 = sums
             r, d = spread(r_ref, x)
             w = r - implicit_diagonal * d
+            return (m1 + fold(r * w), m2 + fold(w * w)), w
+
+        def store_second(x, w):
             keep(w_tag, x, w)
-            return m1 + fold(r * w), m2 + fold(w * w)
-
-        sums = lax.fori_loop(1, nx - 1, second_pass, (nothing, nothing))
+
+        sums = grouped("image", 1, nx - 1, second_pass, store_second, (nothing, nothing))
         arrive(r_tag)
         unpack(r_tag)
-        m1, m2 = second_pass(nx - 1, second_pass(0, sums))
+        for x in (0, nx - 1):
+            sums, w = second_pass(x, sums)
+            store_second(x, w)
+        m1, m2 = sums
         start_x(w_tag)
         for side, face in ((0, yrecv[7, 0]), (1, ysend[7, 1])):
             change = jnp.where(between, -implicit_diagonal * face * yrecv[r_tag, side], 0.0)
@@ -313,8 +347,8 @@
             m2 += fold((2.0 * w + change) * change)
         start_y(w_tag)
         for x in range(1, nx - 1):
-            fields[w_tag, 1 + x, pl.ds(PAD, 1)] = ysend[w_tag, 0, pl.ds(x, 1)]
-            fields[w_tag, 1 + x, pl.ds(PAD + ny - 1, 1)] = ysend[w_tag, 1, pl.ds(x, 1)]
+            fields[w_tag][1 + x, pl.ds(PAD, 1)] = ysend[w_tag, 0, pl.ds(x, 1)]
+            fields[w_tag][1 + x, pl.ds(PAD + ny - 1, 1)] = ysend[w_tag, 1, pl.ds(x, 1)]
 
         def third_pass(x, m3):
             w = w_ref[x + 1, own]
@@ -323,17 +357,16 @@
             jump_z = jnp.where(last_lane, 0.0, ahead_z(w)) - w
             total = cx[x + 1] * jump_x * jump_x + cy[x, own] * jump_y * jump_y
             total += cz[x] * jump_z * jump_z
-            return m3 + fold(total)
-
-        m3 = lax.fori_loop(0, nx - 1, third_pass, nothing)
-
-        def carry_r(x, carry):
-            fr[step, x] = carried(r_ref, x)
-            return carry
-
-        lax.fori_loop(0, nx, carry_r, 0)
+            return m3 + fold(total), None
+
+        m3 = grouped("energy", 0, nx - 1, third_pass, lambda x, kept: None, nothing)
+
+        def store_r(x, kept):
+            fr[step][x] = kept
+
+        grouped("carry", 0, nx, lambda x, c: (c, carried(r_ref, x)), store_r, 0)
         arrive(w_tag)
-        m3 = third_pass(nx - 1, m3)
+        m3, _ = third_pass(nx - 1, m3)
         above = yrecv[w_tag, 1]
         m3 += fold(ysend[7, 1] * above * (above - 2.0 * ysend[w_tag, 1]))
         m3 = m2 + implicit_diagonal * m3
@@ -343,12 +376,10 @@
         pending += out
         unpack(w_tag)
 
-        def carry_w(x, carry):
-            fw[step, x] = carried(w_ref, x)
-            dw[step, x] = spread(w_ref, x)[1]
-            return carry
-
-        lax.fori_loop(0, nx, carry_w, 0)
+        def store_w(x, kept):
+            fw[step][x], dw[step][x] = kept
+
+        grouped("both", 0, nx, lambda x, c: (c, (carried(w_ref, x), spread(w_ref, x)[1])), store_w, 0)
         red_x[step, me_x] = result()
         out, result = across(step, red_x, "gx", me_x, gx, rxs, rxr)
         pending += out
@@ -357,20 +388,22 @@
         share = section_weights[target] / section_weights[3]
 
         def gather(x, carry):
-            total = share * fields[1, x + 1, own]
+            total = share * fields[1][x + 1, own]
             for k in range(step):
-                total += explicit_table[3 - k][target] * fr[k, x] + implicit_table[3 - k][target] * dw[k, x]
+                total += explicit_table[3 - k][target] * fr[k][x] + implicit_table[3 - k][target] * dw[k][x]
             if target == 0:
-                total += fields[0, x + 1, own]
+                total += fields[0][x + 1, own]
                 for k in range(step):
                     on_r, on_w = weights[k]
-                    total += on_r * fields[1 + k, x + 1, own] + on_w * fields[4 + k, x + 1, own]
-            base[x] = total
-            return carry
+                    total += on_r * fields[1 + k][x + 1, own] + on_w * fields[4 + k][x + 1, own]
+            return carry, total
 
         if step == 0:
             weights = []
-        lax.fori_loop(0, nx, gather, 0)
+        def store_base(x, kept):
+            base[x] = kept
+
+        grouped("gather", 0, nx, gather, store_base, 0)
 
         total = result()
         total = jnp.broadcast_to(jnp.sum(total, axis=1, keepdims=True), (8, nz))
@@ -385,17 +418,15 @@
         weights.append((on_r, on_w))
 
         def following(x, step=step, section=section, target=target, on_r=on_r, on_w=on_w):
-            r, w = fields[1 + step, x + 1, own], fields[4 + step, x + 1, own]
-            advected = on_r * fr[step, x] + on_w * fw[step, x]
-            diffused = (on_r / implicit_diagonal) * (r - w) + on_w * dw[step, x]
+            r, w = fields[1 + step][x + 1, own], fields[4 + step][x + 1, own]
+            advected = on_r * fr[step][x] + on_w * fw[step][x]
+            diffused = (on_r / implicit_diagonal) * (r - w) + on_w * dw[step][x]
             total = base[x]
             total += explicit_table[section][target] * advected
             total += implicit_table[section][target] * diffused
             if target == 0:
                 return total + on_r * r + on_w * w
-            fr[step, x] = advected
-            dw[step, x] = diffused
-            return total
+            return total, (advected, diffused)
 
     def last(x, carry):
         out_ref[x] = following(x)
@@ -424,10 +455,8 @@
         in_specs=[anywhere, anywhere, anywhere, pl.BlockSpec(memory_space=pltpu.VMEM)],
         out_specs=pl.BlockSpec(memory_space=pltpu.VMEM),
         scratch_shapes=[
-            pltpu.VMEM((7, nx + 2, rows, nz), f32),
-            pltpu.VMEM((3, nx, ny, nz), f32),
-            pltpu.VMEM((3, nx, ny, nz), f32),
-            pltpu.VMEM((3, nx, ny, nz), f32),
+            *[pltpu.VMEM((nx + 2, rows, nz), f32)] * 7,
+            *[plain] * 9,
             plain,
             pltpu.VMEM((nx + 1, ny, nz), f32),
             pltpu.VMEM((nx, rows, nz), f32),

time: 72.4 us -> 60.4 us (0.83)
  Pallas kernels: 69.9 us -> 57.9 us
    pallas_call x1, Pallas kernels: 69.9 us -> 57.9 us  [local(): pl.pallas_call(functools.partial(kernel, gx, gy), out_shape=jax.ShapeDtyp...]
where the time goes in v3:
time: 60.4 us; the launch traced here: 60.2 us
  Pallas kernels  57.9 us (96%)
  local copies, waits for them, and re-layouts  2.31 us (4%)
    pallas_call x1, Pallas kernels, local(): pl.pallas_call(functools.partial(kernel, gx, gy), out_shape=jax.ShapeDtyp...  57.9 us
    unnamed x1, local copies, waits for them, and re-layouts  2.31 us

profile of v3, /device:TPU:0, one launch (start us, length us, event | category | flops | bytes accessed | tf_op | source)
XLA Modules:
  0.0 60.2 jit_solution(2877154133265353162)
XLA Ops:
  0.0 57.9 %shard_map.46 = f32[32,64,128]{2,1,0:T(8,128)} custom-call(f32[32,64,128]{2,1,0:T(8,128)} %cot_hbm.1, f32[3,32,64,128]{3,2,1,0:T(8,128)} %speed_hbm.1, f32[3,32,64,128]{3,2,1,0:T(8,128)} %coeff_hbm.1, s32[3,32,64]{2,1,0:T(8,128)} %dirs_ref.1), custom_call_target="tpu_custom_call" | custom-call | tf_op jit(solution)/shard_map/pallas_call | solution.py:452
  57.9 2.3 %copy.6 = f32[32,64,128]{2,1,0:T(8,128)} copy(f32[32,64,128]{2,1,0:T(8,128)} %shard_map.46) | data formatting | bytes 2097152
